TPU v7x, 32 devices: a whole 2x2x4 slice. The times are simulated.
32 devices in a mesh: row: 2 (over y), col: 16 (over z, x, core).
Axes of the slice: x: 2, y: 2, z: 4, core: 2. Of those that a mesh axis runs over, the one named last changes fastest.
Arguments:
- image_student: bfloat16 [2048, 1024], P(('row', 'col')), may hold values from -2.5 to 2.5
- text_student: bfloat16 [2048, 1024], P(('col', 'row')), may hold values from -2.5 to 2.5
- image_teacher: bfloat16 [2048, 1024], P(('row', 'col')), may hold values from -2.5 to 2.5
- text_teacher: bfloat16 [2048, 1024], P(('col', 'row')), may hold values from -2.5 to 2.5
Outputs:
- loss: float32 [], replicated
- image_grad: float32 [2048, 1024], P(('row', 'col'))
- text_grad: float32 [2048, 1024], P(('col', 'row'))
All inputs are finite; a program needn't handle non-finite values.
Results may differ from a plain program's by a relative error of at most 0.002.
Values may be sent and summed in bfloat16 or wider, within the bound.
A program may use at most 128 MiB of HBM per device.

v0:
```python
import jax
import jax.numpy as jnp
from jax import lax
from jax.sharding import PartitionSpec as P

logit_scale = 100.0


def joined(value, axis, join):
    pieces = jax.tree.map(lambda part: lax.all_gather(part, axis), value)
    head = jax.tree.map(lambda part: part[0], pieces)
    tail = jax.tree.map(lambda part: part[1:], pieces)
    subtotal, _ = lax.scan(lambda subtotal, slab: (join(subtotal, slab), None), head, tail)
    return subtotal


def tile_logits(left, right):
    return logit_scale * lax.dot_general(
        left, right, (((1,), (1,)), ((), ())), preferred_element_type=jnp.float32
    )


def partial_stats(student, teacher, along):
    student_high = jnp.max(student, along, keepdims=True)
    student_total = jnp.sum(jnp.exp(student - student_high), along)
    teacher_high = jnp.max(teacher, along, keepdims=True)
    weights = jnp.exp(teacher - teacher_high)
    teacher_total = jnp.sum(weights, along)
    divergence = jnp.sum(weights * (teacher - student), along)
    return (
        jnp.squeeze(student_high, along),
        student_total,
        jnp.squeeze(teacher_high, along),
        teacher_total,
        divergence,
    )


def merge_stats(first, second):
    student_high = jnp.maximum(first[0], second[0])
    teacher_high = jnp.maximum(first[2], second[2])
    early = jnp.exp(first[2] - teacher_high)
    later = jnp.exp(second[2] - teacher_high)
    student_total = first[1] * jnp.exp(first[0] - student_high) + second[1] * jnp.exp(
        second[0] - student_high
    )
    return (
        student_high,
        student_total,
        teacher_high,
        first[3] * early + second[3] * later,
        first[4] * early + second[4] * later,
    )


def finish(stats):
    student_lse = stats[0] + jnp.log(stats[1])
    teacher_lse = stats[2] + jnp.log(stats[3])
    divergence = stats[4] / stats[3] - teacher_lse + student_lse
    return (student_lse, teacher_lse, 0.5 * (student_lse + divergence))


def body(image_student, text_student, image_teacher, text_teacher):
    per_device = image_student.shape[0]
    image_slab, image_frozen = (
        lax.all_gather(image_student, "col", axis=0, tiled=True),
        lax.all_gather(image_teacher, "col", axis=0, tiled=True),
    )
    text_slab, text_frozen = (
        lax.all_gather(text_student, "row", axis=0, tiled=True),
        lax.all_gather(text_teacher, "row", axis=0, tiled=True),
    )
    student = tile_logits(image_slab, text_slab)
    teacher = tile_logits(image_frozen, text_frozen)
    row_stats = joined(partial_stats(student, teacher, 1), "col", merge_stats)
    column_stats = joined(partial_stats(student, teacher, 0), "row", merge_stats)
    student_rows, teacher_rows, row_terms = finish(row_stats)
    student_columns, teacher_columns, column_terms = finish(column_stats)
    row_place = lax.axis_index("row")
    col_place = lax.axis_index("col")
    row_index = row_place * student.shape[0] + jnp.arange(student.shape[0], dtype=jnp.int32)
    column_index = col_place * student.shape[1] + jnp.arange(student.shape[1], dtype=jnp.int32)
    identity = (row_index[:, None] == column_index[None, :]).astype(jnp.float32)
    own_rows = lax.dynamic_slice_in_dim(row_terms, col_place * per_device, per_device)
    own_columns = lax.dynamic_slice_in_dim(column_terms, row_place * per_device, per_device)
    partial_value = jnp.sum(own_rows) + jnp.sum(own_columns) - jnp.sum(student * identity)
    pair_count = per_device * lax.axis_size("row") * lax.axis_size("col")
    loss = lax.psum(partial_value, ("row", "col")) / pair_count
    gradient = (
        jnp.exp(student - student_rows[:, None])
        + jnp.exp(student - student_columns[None, :])
        - 0.5
        * (jnp.exp(teacher - teacher_rows[:, None]) + jnp.exp(teacher - teacher_columns[None, :]))
        - identity
    ).astype(jnp.bfloat16)
    picked = gradient
    image_grad = lax.psum_scatter(
        logit_scale * jnp.dot(picked, text_slab, preferred_element_type=jnp.float32),
        "col",
        scatter_dimension=0,
        tiled=True,
    )
    picked = gradient
    text_grad = lax.psum_scatter(
        logit_scale
        * lax.dot_general(
            picked, image_slab, (((0,), (0,)), ((), ())), preferred_element_type=jnp.float32
        ),
        "row",
        scatter_dimension=0,
        tiled=True,
    )
    return (loss, image_grad, text_grad)


def solution(mesh):
    return jax.shard_map(
        body,
        mesh=mesh,
        in_specs=(
            P(("row", "col"), None),
            P(("col", "row"), None),
            P(("row", "col"), None),
            P(("col", "row"), None),
        ),
        out_specs=(P(), P(("row", "col"), None), P(("col", "row"), None)),
        check_vma=False,
    )
```

profile of v0, /device:TPU:0, one launch (start us, length us, event | category | flops | bytes accessed | tf_op | source)
XLA Modules:
  0.0 348.5 jit_solution(8966833049292975787)
XLA Ops:
  8.7 7.4 %all_gather.61 = bf16[128,1024]{1,0:T(8,128)(2,1)S(1)} all-gather(bf16[64,1024]{1,0:T(8,128)(2,1)} %param.7), channel_id=1, replica_groups=mesh['row'=2,'col'=16] {'row'}, dimensions={0}, use_global_device_ids=true | all-gather | bytes 393216 | tf_op jit(solution)/shard_map/all_gather | solution.py:70
  16.1 5.8 %all_gather.66 = bf16[128,1024]{1,0:T(8,128)(2,1)S(1)} all-gather(bf16[64,1024]{1,0:T(8,128)(2,1)} %param.9), channel_id=1, replica_groups=mesh['row'=2,'col'=16] {'row'}, dimensions={0}, use_global_device_ids=true | all-gather | bytes 393216 | tf_op jit(solution)/shard_map/all_gather | solution.py:71
  22.5 31.8 %all-gather.20.cloned.1.call-done = bf16[1024,1024]{1,0:T(8,128)(2,1)} async-done(((bf16[64,1024]{1,0:T(8,128)(2,1)}), bf16[1024,1024]{1,0:T(8,128)(2,1)}) %all-gather.20.cloned.1.call-update) | async-done | bytes 2097168 | tf_op jit(solution)/shard_map/all_gather | solution.py:67
  54.3 2.9 fusion.37
  57.2 19.3 %all-gather.2 = f32[16384]{0:T(1024)S(1)} all-gather(f32[1024]{0:T(1024)S(1)} %get-tuple-element.112), channel_id=4, replica_groups=mesh['row'=2,'col'=16] {'col'}, dimensions={0}, use_global_device_ids=true | all-gather | bytes 69632 | tf_op jit(solution)/shard_map/all_gather | solution.py:10
  76.5 20.5 %all-gather.18.cloned.1.call-done = bf16[1024,1024]{1,0:T(8,128)(2,1)} async-done(((bf16[64,1024]{1,0:T(8,128)(2,1)}), bf16[1024,1024]{1,0:T(8,128)(2,1)}) %all-gather.18.cloned.1.call-update) | async-done | bytes 2097168 | tf_op jit(solution)/shard_map/all_gather | solution.py:66
  97.0 2.4 fusion.36
  99.4 19.4 %all-gather = f32[16384]{0:T(1024)S(1)} all-gather(f32[1024]{0:T(1024)S(1)} %get-tuple-element.110), channel_id=2, replica_groups=mesh['row'=2,'col'=16] {'col'}, dimensions={0}, use_global_device_ids=true | all-gather | bytes 69632 | tf_op jit(solution)/shard_map/all_gather | solution.py:10
  118.8 2.5 multiply_reduce_fusion
  121.4 17.6 %all-gather.4 = f32[16384]{0:T(1024)S(1)} all-gather(f32[1024]{0:T(1024)S(1)} %get-tuple-element.103), channel_id=6, replica_groups=mesh['row'=2,'col'=16] {'col'}, dimensions={0}, use_global_device_ids=true | all-gather | bytes 69632 | tf_op jit(solution)/shard_map/all_gather | solution.py:10
  139.6 18.9 %all-gather.3 = f32[16384]{0:T(1024)S(1)} all-gather(f32[1024]{0:T(1024)S(1)} %get-tuple-element.104), channel_id=5, replica_groups=mesh['row'=2,'col'=16] {'col'}, dimensions={0}, use_global_device_ids=true | all-gather | bytes 69632 | tf_op jit(solution)/shard_map/all_gather | solution.py:10
  159.1 17.6 %all-gather.1 = f32[16384]{0:T(1024)S(1)} all-gather(f32[1024]{0:T(1024)S(1)} %get-tuple-element.108), channel_id=3, replica_groups=mesh['row'=2,'col'=16] {'col'}, dimensions={0}, use_global_device_ids=true | all-gather | bytes 69632 | tf_op jit(solution)/shard_map/all_gather | solution.py:10
  177.4 4.2 %all-gather.13 = f32[2,1,128]{2,1,0:T(1,128)} all-gather(f32[1,1,128]{2,1,0:T(1,128)S(1)} %bitcast.195), channel_id=10, replica_groups=mesh['row'=2,'col'=16] {'row'}, dimensions={0}, use_global_device_ids=true | all-gather | bytes 1536 | tf_op jit(solution)/shard_map/all_gather | solution.py:10
  182.2 4.4 %all-gather.10 = f32[2,1,128]{2,1,0:T(1,128)S(1)} all-gather(f32[1,1,128]{2,1,0:T(1,128)} %bitcast.196), channel_id=7, replica_groups=mesh['row'=2,'col'=16] {'row'}, dimensions={0}, use_global_device_ids=true | all-gather | bytes 1536 | tf_op jit(solution)/shard_map/all_gather | solution.py:10
  186.6 4.4 %all-gather.14 = f32[2,1,128]{2,1,0:T(1,128)S(1)} all-gather(f32[1,1,128]{2,1,0:T(1,128)} %bitcast.199), channel_id=11, replica_groups=mesh['row'=2,'col'=16] {'row'}, dimensions={0}, use_global_device_ids=true | all-gather | bytes 1536 | tf_op jit(solution)/shard_map/all_gather | solution.py:10
  191.0 4.3 %all-gather.11 = f32[2,1,128]{2,1,0:T(1,128)S(1)} all-gather(f32[1,1,128]{2,1,0:T(1,128)} %bitcast.198), channel_id=8, replica_groups=mesh['row'=2,'col'=16] {'row'}, dimensions={0}, use_global_device_ids=true | all-gather | bytes 1536 | tf_op jit(solution)/shard_map/all_gather | solution.py:10
  195.9 0.8 reshape.44
  196.7 1.5 reshape.43
  198.2 1.5 reshape.41
  199.7 47.1 %while.2 = (s32[]{:T(128)}, f32[1024]{0:T(1024)S(1)}, f32[1024]{0:T(1024)S(1)}, f32[1024]{0:T(1024)S(1)}, f32[1024]{0:T(1024)S(1)}, /*index=5*/f32[1024]{0:T(102...) while((s32[]{:T(128)}, f32[1024]{0:T(1024)S(1)}, ...), condition=%wide.region_6.7_spmd, body=%wide.region_5.6_spmd.sunk | while | flops 17410 | bytes 123025 | solution.py:13
  199.7 0.8 constant_dynamic-slice_fusion.14
  200.5 0.8 constant_dynamic-slice_fusion.11
  201.2 0.8 constant_dynamic-slice_fusion.12
  202.0 0.8 constant_dynamic-slice_fusion.13
  202.8 0.8 constant_dynamic-slice_fusion.14
  203.6 0.8 constant_dynamic-slice_fusion.11
  204.4 0.8 constant_dynamic-slice_fusion.12
  205.1 0.8 constant_dynamic-slice_fusion.13
  206.0 0.8 constant_dynamic-slice_fusion.14
  206.7 0.8 constant_dynamic-slice_fusion.11
  207.5 0.8 constant_dynamic-slice_fusion.12
  208.3 0.8 constant_dynamic-slice_fusion.13
  209.1 0.8 constant_dynamic-slice_fusion.14
  209.9 0.8 constant_dynamic-slice_fusion.11
  210.6 0.8 constant_dynamic-slice_fusion.12
  211.4 0.8 constant_dynamic-slice_fusion.13
  212.3 0.8 constant_dynamic-slice_fusion.14
  213.0 0.8 constant_dynamic-slice_fusion.11
  213.8 0.8 constant_dynamic-slice_fusion.12
  214.6 0.8 constant_dynamic-slice_fusion.13
  215.4 0.8 constant_dynamic-slice_fusion.14
  216.2 0.8 constant_dynamic-slice_fusion.11
  216.9 0.8 constant_dynamic-slice_fusion.12
  217.7 0.8 constant_dynamic-slice_fusion.13
  218.5 0.8 constant_dynamic-slice_fusion.14
  219.3 0.8 constant_dynamic-slice_fusion.11
  220.1 0.8 constant_dynamic-slice_fusion.12
  221.7 0.8 constant_dynamic-slice_fusion.14
  224.8 0.8 constant_dynamic-slice_fusion.14
  225.6 0.8 constant_dynamic-slice_fusion.11
  227.1 0.8 constant_dynamic-slice_fusion.13
  228.0 0.8 constant_dynamic-slice_fusion.14
  231.1 0.8 constant_dynamic-slice_fusion.14
  232.6 0.8 constant_dynamic-slice_fusion.12
  234.2 0.8 constant_dynamic-slice_fusion.14
  237.4 0.8 constant_dynamic-slice_fusion.14
  238.2 0.8 constant_dynamic-slice_fusion.11
  240.5 0.8 constant_dynamic-slice_fusion.14
  243.7 0.8 constant_dynamic-slice_fusion.14
  247.5 2.7 convolution_multiply_fusion.1
  250.3 2.7 convolution_multiply_fusion
  253.6 4.2 %all-gather.12 = f32[2,1,128]{2,1,0:T(1,128)S(1)} all-gather(f32[1,1,128]{2,1,0:T(1,128)S(1)} %bitcast.197), channel_id=9, replica_groups=mesh['row'=2,'col'=16] {'row'}, dimensions={0}, use_global_device_ids=true | all-gather | bytes 1536 | tf_op jit(solution)/shard_map/all_gather | solution.py:10
  261.0 38.3 %psum.7 = f32[]{:T(128)} all-reduce(f32[]{:T(128)S(6)} %sub.142), channel_id=1, replica_groups=mesh['row'=2,'col'=16] {'row','col'}, use_global_device_ids=true, to_apply=%region_15.16 | all-reduce | flops 1 | bytes 8 | tf_op jit(solution)/shard_map/psum | solution.py:88
  300.0 40.8 %reduce-scatter.3.cloned.1.call-done = f32[64,1024]{1,0:T(8,128)} async-done(((f32[1024,1024]{1,0:T(8,128)}), f32[64,1024]{1,0:T(8,128)}) %reduce-scatter.3.cloned.1.call-update) | async-done | bytes 262160 | tf_op jit(solution)/shard_map/reduce_scatter | solution.py:97
  (122 shorter events, 24.6 us)
Async XLA Ops:
  7.2 47.2 %all-gather.20.cloned.1.call-start = ((), (), s32[]{:S(2)}) async-start(), calls=%async_computation.3 | async-start | bytes 2228224 | tf_op jit(solution)/shard_map/all_gather | solution.py:67
  7.9 89.1 %all-gather.18.cloned.1.call-start = ((), (), s32[]{:S(2)}) async-start(), calls=%async_computation.2 | async-start | bytes 2228224 | tf_op jit(solution)/shard_map/all_gather | solution.py:66
  8.6 291.4 %reduce-scatter.5.cloned.1.call-start = ((), (), s32[]{:S(2)}) async-start(), calls=%async_computation.5 | async-start | bytes 786432 | tf_op jit(solution)/shard_map/reduce_scatter | solution.py:104
  97.0 21.9 %copy-start.3 = (f32[128]{0:T(128)S(1)}, f32[128]{0:T(128)}, u32[]{:S(2)}) copy-start(f32[128]{0:T(128)} %get-tuple-element.111) | copy-start | bytes 1540
  99.4 78.0 %copy-start.4 = (f32[128]{0:T(128)}, f32[128]{0:T(128)S(1)}, u32[]{:S(2)}) copy-start(f32[128]{0:T(128)S(1)} %get-tuple-element.109) | copy-start | bytes 1540
  99.4 148.1 %copy-start = (bf16[1024,1024]{1,0:T(8,128)(2,1)S(1)}, bf16[1024,1024]{1,0:T(8,128)(2,1)}, u32[]{:S(2)}) copy-start(bf16[1024,1024]{1,0:T(8,128)(2,1)} %all-gather.18.cloned.1.call-done) | copy-start | bytes 6291460
  247.5 2.8 copy-start.1
  250.3 90.6 %reduce-scatter.3.cloned.1.call-start = ((), (), s32[]{:S(2)}) async-start(), calls=%async_computation.4 | async-start | bytes 4456448 | tf_op jit(solution)/shard_map/reduce_scatter | solution.py:97
  253.0 0.6 copy-start.5
  253.0 4.8 %copy-start.2 = (f32[2,1,128]{2,1,0:T(1,128)S(1)}, f32[2,1,128]{2,1,0:T(1,128)}, u32[]{:S(2)}) copy-start(f32[2,1,128]{2,1,0:T(1,128)} %all-gather.13) | copy-start | bytes 3076
Sparse Core Ops, SparseCore 0:
  10.1 44.1 all-gather.19
  56.5 40.4 all-gather.17
  250.4 13.1 reduce-scatter.4
  267.8 72.9 reduce-scatter.2
where the time goes:
time: 353 us; the launch traced here: 348 us
  blocking collectives  166 us (47%)
  waiting for transfers between devices  94.5 us (27%)
  local copies, waits for them, and re-layouts  53.7 us (15%)
  between operations  17.5 us (5%)
  matrix products  10.7 us (3%)
  other arithmetic  5.52 us (2%)
    all_gather x10, blocking collectives, joined(): pieces = jax.tree.map(lambda part: lax.all_gather(part, axis), value)  114 us
    dynamic_slice x75, local copies, waits for them, and re-layouts, joined(): lax.scan(lambda subtotal, slab: (join(subtotal, slab), None), head, tail)  46.1 us
    reduce_scatter x1, waiting for transfers between devices, body(): lax.psum_scatter(logit_scale * jnp.dot(picked, text_slab, preferred_eleme...  40.8 us
    psum x1, blocking collectives, body(): loss = lax.psum(partial_value, ('row', 'col')) / pair_count  38.3 us
    all_gather x1, waiting for transfers between devices, body(): lax.all_gather(image_teacher, 'col', axis=0, tiled=True)  31.8 us
    all_gather x1, waiting for transfers between devices, body(): lax.all_gather(image_student, 'col', axis=0, tiled=True)  20.5 us
    all_gather x1, blocking collectives, body(): lax.all_gather(text_student, 'row', axis=0, tiled=True)  7.42 us
  transfers between devices with their start and end apart: 4, of which 3 were waited for; matrix products, arithmetic and copies ran while one was open for 2% of the time, Pallas kernels for 0%

commit v1 on v0

--- a/solution.py
+++ b/solution.py
@@ -64,7 +64,9 @@
     per_device = image_student.shape[0]
     image_slab, image_frozen = (
         lax.all_gather(image_student, "col", axis=0, tiled=True),
-        lax.all_gather(image_teacher, "col", axis=0, tiled=True),
+        jnp.concatenate(
+            lax.all_to_all(jnp.stack([image_teacher] * lax.axis_size("col")), "col", 0, 0), axis=0
+        ),
     )
     text_slab, text_frozen = (
         lax.all_gather(text_student, "row", axis=0, tiled=True),

time: 353 us -> 352 us (level)
  starting transfers between devices: 0.16 us -> 7.64 us
  waiting for transfers between devices: 94.5 us -> 89.6 us
    all_to_all x0 -> x1, waiting for transfers between devices: none -> 32.3 us  [body(): lax.all_to_all(jnp.stack([image_teacher] * lax.axis_size('col')), 'col',...]
    all_gather x1 -> x0, waiting for transfers between devices: 31.8 us -> none  [body(): lax.all_gather(image_teacher, 'col', axis=0, tiled=True)]
    all_to_all x0 -> x1, starting transfers between devices: none -> 7.52 us  [body(): lax.all_to_all(jnp.stack([image_teacher] * lax.axis_size('col')), 'col',...]
    all_gather x1, waiting for transfers between devices: 20.5 us -> 15.7 us  [body(): lax.all_gather(image_student, 'col', axis=0, tiled=True)]
  transfers between devices with their start and end apart: 4 -> 4, of which waited for: 3 -> 3; matrix products, arithmetic and copies ran while one was open for 2% -> 1% of each run, Pallas kernels for 0% -> 0%
where the time goes in v1:
time: 352 us; the launch traced here: 347 us
  blocking collectives  164 us (47%)
  waiting for transfers between devices  89.6 us (25%)
  local copies, waits for them, and re-layouts  56.3 us (16%)
  between operations  17.5 us (5%)
  matrix products  8.49 us (2%)
  starting transfers between devices  7.64 us (2%)
  other arithmetic  3.59 us (1%)
    all_gather x10, blocking collectives, joined(): pieces = jax.tree.map(lambda part: lax.all_gather(part, axis), value)  115 us
    dynamic_slice x75, local copies, waits for them, and re-layouts, joined(): lax.scan(lambda subtotal, slab: (join(subtotal, slab), None), head, tail)  46.2 us
    reduce_scatter x1, waiting for transfers between devices, body(): lax.psum_scatter(logit_scale * jnp.dot(picked, text_slab, preferred_eleme...  41 us
    psum x1, blocking collectives, body(): loss = lax.psum(partial_value, ('row', 'col')) / pair_count  36.8 us
    all_to_all x1, waiting for transfers between devices, body(): lax.all_to_all(jnp.stack([image_teacher] * lax.axis_size('col')), 'col',...  32.3 us
    all_gather x1, waiting for transfers between devices, body(): lax.all_gather(image_student, 'col', axis=0, tiled=True)  15.7 us
    all_to_all x1, starting transfers between devices, body(): lax.all_to_all(jnp.stack([image_teacher] * lax.axis_size('col')), 'col',...  7.52 us
  transfers between devices with their start and end apart: 4, of which 3 were waited for; matrix products, arithmetic and copies ran while one was open for 1% of the time, Pallas kernels for 0%

profile of v1, /device:TPU:0, one launch (start us, length us, event | category | flops | bytes accessed | tf_op | source)
XLA Modules:
  0.0 347.2 jit_solution(6357916014280418535)
XLA Ops:
  7.2 2.5 stack.2
  9.6 7.5 %all-to-all-start = ((bf16[16,64,1024]{2,1,0:T(8,128)(2,1)}), bf16[16,64,1024]{2,1,0:T(8,128)(2,1)S(1)}, u32[]{:S(2)}, u32[]{:S(2)}) async-start(bf16[16,64,1024]{2,1,0:T(8,128)(2,1)} %stack.2), calls=%async_computation | async-start | bytes 4194304 | tf_op jit(solution)/shard_map/all_to_all | solution.py:68
  18.0 6.5 %all_gather.58 = bf16[128,1024]{1,0:T(8,128)(2,1)S(1)} all-gather(bf16[64,1024]{1,0:T(8,128)(2,1)S(1)} %copy-done.1), channel_id=1, replica_groups=mesh['row'=2,'col'=16] {'row'}, dimensions={0}, use_global_device_ids=true | all-gather | bytes 393216 | tf_op jit(solution)/shard_map/all_gather | solution.py:72
  24.4 5.6 %all_gather.62 = bf16[128,1024]{1,0:T(8,128)(2,1)S(1)} all-gather(bf16[64,1024]{1,0:T(8,128)(2,1)S(1)} %copy-done.2), channel_id=1, replica_groups=mesh['row'=2,'col'=16] {'row'}, dimensions={0}, use_global_device_ids=true | all-gather | bytes 393216 | tf_op jit(solution)/shard_map/all_gather | solution.py:73
  30.1 32.3 %all-to-all-done = bf16[16,64,1024]{2,1,0:T(8,128)(2,1)S(1)} async-done(((bf16[16,64,1024]{2,1,0:T(8,128)(2,1)}), bf16[16,64,1024]{2,1,0:T(8,128)(2,1)S(1)}, u32[]{:S(2)}, u32[]{:S(2)}) %all-to-all-start) | async-done | bytes 2097184 | tf_op jit(solution)/shard_map/all_to_all | solution.py:68
  62.3 0.8 fusion.37
  63.1 15.7 %all-gather.17.cloned.1.call-done = bf16[1024,1024]{1,0:T(8,128)(2,1)} async-done(((bf16[64,1024]{1,0:T(8,128)(2,1)}), bf16[1024,1024]{1,0:T(8,128)(2,1)}) %all-gather.17.cloned.1.call-update) | async-done | bytes 2097168 | tf_op jit(solution)/shard_map/all_gather | solution.py:66
  78.8 2.4 fusion.36
  81.2 1.9 multiply_reduce_fusion
  83.1 19.8 %all-gather.1 = f32[16384]{0:T(1024)S(1)} all-gather(f32[1024]{0:T(1024)S(1)} %get-tuple-element.108), channel_id=3, replica_groups=mesh['row'=2,'col'=16] {'col'}, dimensions={0}, use_global_device_ids=true | all-gather | bytes 69632 | tf_op jit(solution)/shard_map/all_gather | solution.py:10
  102.9 17.6 %all-gather.3 = f32[16384]{0:T(1024)S(1)} all-gather(f32[1024]{0:T(1024)S(1)} %get-tuple-element.104), channel_id=5, replica_groups=mesh['row'=2,'col'=16] {'col'}, dimensions={0}, use_global_device_ids=true | all-gather | bytes 69632 | tf_op jit(solution)/shard_map/all_gather | solution.py:10
  120.5 18.9 %all-gather.4 = f32[16384]{0:T(1024)S(1)} all-gather(f32[1024]{0:T(1024)S(1)} %get-tuple-element.103), channel_id=6, replica_groups=mesh['row'=2,'col'=16] {'col'}, dimensions={0}, use_global_device_ids=true | all-gather | bytes 69632 | tf_op jit(solution)/shard_map/all_gather | solution.py:10
  140.1 17.7 %all-gather = f32[16384]{0:T(1024)S(1)} all-gather(f32[1024]{0:T(1024)S(1)} %get-tuple-element.110), channel_id=2, replica_groups=mesh['row'=2,'col'=16] {'col'}, dimensions={0}, use_global_device_ids=true | all-gather | bytes 69632 | tf_op jit(solution)/shard_map/all_gather | solution.py:10
  158.3 18.8 %all-gather.2 = f32[16384]{0:T(1024)S(1)} all-gather(f32[1024]{0:T(1024)S(1)} %get-tuple-element.112), channel_id=4, replica_groups=mesh['row'=2,'col'=16] {'col'}, dimensions={0}, use_global_device_ids=true | all-gather | bytes 69632 | tf_op jit(solution)/shard_map/all_gather | solution.py:10
  179.1 0.8 reshape.50
  179.9 1.5 reshape.46
  181.4 1.5 reshape.48
  182.9 47.0 %while.2 = (s32[]{:T(128)}, f32[1024]{0:T(1024)S(1)}, f32[1024]{0:T(1024)S(1)}, f32[1024]{0:T(1024)S(1)}, f32[1024]{0:T(1024)S(1)}, /*index=5*/f32[1024]{0:T(102...) while((s32[]{:T(128)}, f32[1024]{0:T(1024)S(1)}, ...), condition=%wide.region_6.7_spmd, body=%wide.region_5.6_spmd.sunk | while | flops 17410 | bytes 123017 | solution.py:13
  183.6 0.8 constant_dynamic-slice_fusion.12
  185.2 0.8 constant_dynamic-slice_fusion.14
  186.0 0.8 constant_dynamic-slice_fusion.11
  186.8 0.8 constant_dynamic-slice_fusion.12
  188.3 0.8 constant_dynamic-slice_fusion.14
  189.1 0.8 constant_dynamic-slice_fusion.11
  189.9 0.8 constant_dynamic-slice_fusion.12
  191.4 0.8 constant_dynamic-slice_fusion.14
  192.3 0.8 constant_dynamic-slice_fusion.11
  193.0 0.8 constant_dynamic-slice_fusion.12
  194.6 0.8 constant_dynamic-slice_fusion.14
  195.4 0.8 constant_dynamic-slice_fusion.11
  196.2 0.8 constant_dynamic-slice_fusion.12
  197.7 0.8 constant_dynamic-slice_fusion.14
  198.5 0.8 constant_dynamic-slice_fusion.11
  199.3 0.8 constant_dynamic-slice_fusion.12
  200.9 0.8 constant_dynamic-slice_fusion.14
  201.7 0.8 constant_dynamic-slice_fusion.11
  202.4 0.8 constant_dynamic-slice_fusion.12
  204.0 0.8 constant_dynamic-slice_fusion.14
  204.8 0.8 constant_dynamic-slice_fusion.11
  205.6 0.8 constant_dynamic-slice_fusion.12
  207.1 0.8 constant_dynamic-slice_fusion.14
  208.7 0.8 constant_dynamic-slice_fusion.12
  210.3 0.8 constant_dynamic-slice_fusion.14
  211.8 0.8 constant_dynamic-slice_fusion.12
  213.4 0.8 constant_dynamic-slice_fusion.14
  215.0 0.8 constant_dynamic-slice_fusion.12
  216.5 0.8 constant_dynamic-slice_fusion.14
  218.1 0.8 constant_dynamic-slice_fusion.12
  219.7 0.8 constant_dynamic-slice_fusion.14
  221.3 0.8 constant_dynamic-slice_fusion.12
  222.8 0.8 constant_dynamic-slice_fusion.14
  224.4 0.8 constant_dynamic-slice_fusion.12
  225.9 0.8 constant_dynamic-slice_fusion.14
  227.5 0.8 constant_dynamic-slice_fusion.12
  229.1 0.8 constant_dynamic-slice_fusion.14
  229.9 4.3 %all-gather.11 = f32[2,1,128]{2,1,0:T(1,128)S(1)} all-gather(f32[1,1,128]{2,1,0:T(1,128)} %bitcast.201), channel_id=8, replica_groups=mesh['row'=2,'col'=16] {'row'}, dimensions={0}, use_global_device_ids=true | all-gather | bytes 1536 | tf_op jit(solution)/shard_map/all_gather | solution.py:10
  234.2 4.4 %all-gather.10 = f32[2,1,128]{2,1,0:T(1,128)S(1)} all-gather(f32[1,1,128]{2,1,0:T(1,128)} %bitcast.198), channel_id=7, replica_groups=mesh['row'=2,'col'=16] {'row'}, dimensions={0}, use_global_device_ids=true | all-gather | bytes 1536 | tf_op jit(solution)/shard_map/all_gather | solution.py:10
  238.6 4.4 %all-gather.14 = f32[2,1,128]{2,1,0:T(1,128)S(1)} all-gather(f32[1,1,128]{2,1,0:T(1,128)} %bitcast.200), channel_id=11, replica_groups=mesh['row'=2,'col'=16] {'row'}, dimensions={0}, use_global_device_ids=true | all-gather | bytes 1536 | tf_op jit(solution)/shard_map/all_gather | solution.py:10
  243.0 4.3 %all-gather.13 = f32[2,1,128]{2,1,0:T(1,128)S(1)} all-gather(f32[1,1,128]{2,1,0:T(1,128)} %bitcast.197), channel_id=10, replica_groups=mesh['row'=2,'col'=16] {'row'}, dimensions={0}, use_global_device_ids=true | all-gather | bytes 1536 | tf_op jit(solution)/shard_map/all_gather | solution.py:10
  247.4 2.6 convolution_multiply_fusion.1
  250.1 2.7 convolution_multiply_fusion
  253.5 4.4 %all-gather.12 = f32[2,1,128]{2,1,0:T(1,128)S(1)} all-gather(f32[1,1,128]{2,1,0:T(1,128)S(1)} %bitcast.199), channel_id=9, replica_groups=mesh['row'=2,'col'=16] {'row'}, dimensions={0}, use_global_device_ids=true | all-gather | bytes 1536 | tf_op jit(solution)/shard_map/all_gather | solution.py:10
  261.0 36.8 %psum.7 = f32[]{:T(128)} all-reduce(f32[]{:T(128)S(6)} %sub.142), channel_id=1, replica_groups=mesh['row'=2,'col'=16] {'row','col'}, use_global_device_ids=true, to_apply=%region_15.16 | all-reduce | flops 1 | bytes 8 | tf_op jit(solution)/shard_map/psum | solution.py:90
  298.5 41.0 %reduce-scatter.3.cloned.1.call-done = f32[64,1024]{1,0:T(8,128)} async-done(((f32[1024,1024]{1,0:T(8,128)}), f32[64,1024]{1,0:T(8,128)}) %reduce-scatter.3.cloned.1.call-update) | async-done | bytes 262160 | tf_op jit(solution)/shard_map/reduce_scatter | solution.py:99
  (126 shorter events, 24.1 us)
Async XLA Ops:
  9.6 8.3 %copy-start.1 = (bf16[64,1024]{1,0:T(8,128)(2,1)S(1)}, bf16[64,1024]{1,0:T(8,128)(2,1)}, u32[]{:S(2)}) copy-start(bf16[64,1024]{1,0:T(8,128)(2,1)} %param.7) | copy-start | bytes 393220
  9.6 14.8 %copy-start.2 = (bf16[64,1024]{1,0:T(8,128)(2,1)S(1)}, bf16[64,1024]{1,0:T(8,128)(2,1)}, u32[]{:S(2)}) copy-start(bf16[64,1024]{1,0:T(8,128)(2,1)} %param.9) | copy-start | bytes 393220
  9.6 52.7 %all-to-all-start = ((bf16[16,64,1024]{2,1,0:T(8,128)(2,1)}), bf16[16,64,1024]{2,1,0:T(8,128)(2,1)S(1)}, u32[]{:S(2)}, u32[]{:S(2)}) async-start(bf16[16,64,1024]{2,1,0:T(8,128)(2,1)} %stack.2), calls=%async_computation | async-start | bytes 4194304 | tf_op jit(solution)/shard_map/all_to_all | solution.py:68
  17.2 61.6 %all-gather.17.cloned.1.call-start = ((), (), s32[]{:S(2)}) async-start(), calls=%async_computation.3 | async-start | bytes 2228224 | tf_op jit(solution)/shard_map/all_gather | solution.py:66
  17.9 280.6 %reduce-scatter.5.cloned.1.call-start = ((), (), s32[]{:S(2)}) async-start(), calls=%async_computation.5 | async-start | bytes 786432 | tf_op jit(solution)/shard_map/reduce_scatter | solution.py:106
  30.1 51.1 %copy-start.3 = (s32[128]{0:T(128)}, s32[128]{0:T(128)S(1)}, u32[]{:S(2)}) copy-start(s32[128]{0:T(128)S(1)} %iota_add_fusion.1) | copy-start | bytes 1540
  63.1 19.9 %copy-start.5 = (f32[128]{0:T(128)}, f32[128]{0:T(128)S(1)}, u32[]{:S(2)}) copy-start(f32[128]{0:T(128)S(1)} %get-tuple-element.111) | copy-start | bytes 1540
  81.2 1.9 copy-start.6
  81.2 166.2 %copy-start = (bf16[1024,1024]{1,0:T(8,128)(2,1)S(1)}, bf16[1024,1024]{1,0:T(8,128)(2,1)}, u32[]{:S(2)}) copy-start(bf16[1024,1024]{1,0:T(8,128)(2,1)} %all-gather.17.cloned.1.call-done) | copy-start | bytes 6291460
  247.4 2.7 copy-start.4
  250.0 89.5 %reduce-scatter.3.cloned.1.call-start = ((), (), s32[]{:S(2)}) async-start(), calls=%async_computation.4 | async-start | bytes 4456448 | tf_op jit(solution)/shard_map/reduce_scatter | solution.py:99
  252.8 0.7 copy-start.7
Sparse Core Ops, SparseCore 0:
  20.1 58.6 all-gather.16
  250.1 11.9 reduce-scatter.4
  266.5 72.9 reduce-scatter.2
